TPU v7x, 32 devices: a whole 2x2x4 slice. The times are simulated.
32 devices in a mesh: dp: 2 (over x), expert: 16 (over z, y, core).
Axes of the slice: x: 2, y: 2, z: 4, core: 2. Of those that a mesh axis runs over, the one named last changes fastest.
Arguments:
- tokens: bfloat16 [4096, 2880], P('expert'), may hold values from -2 to 2
- segment_ids: int32 [4096], P('expert'), may hold values from 0 to 31, never falling along the last dimension, each value on 1 to 512 neighbouring positions
- expert_ids: int32 [4096, 4], P('expert'), may hold values from 0 to 15, as said below
- attn_gain: float32 [2880], replicated, may hold values from 0.1 to 1.9
- sinks: float32 [32], P('dp'), may hold values from 2 to 5
- qkv_master: float32 [2560, 2880], P(('dp', 'expert')), may hold values from -0.109375 to 0.109375
- qkv_mom: float32 [2560, 2880], P(('dp', 'expert')), may hold values from -0.006 to 0.006
- qkv_var: float32 [2560, 2880], P(('dp', 'expert')), may hold values from 1e-08 to 1e-06
- qkv_grad: float32 [2560, 2880], P(('dp', 'expert')), may hold values from -0.06 to 0.06
- o_master: float32 [2048, 2880], P(('dp', 'expert')), may hold values from -0.125 to 0.125
- o_mom: float32 [2048, 2880], P(('dp', 'expert')), may hold values from -0.006 to 0.006
- o_var: float32 [2048, 2880], P(('dp', 'expert')), may hold values from 1e-08 to 1e-06
- o_grad: float32 [2048, 2880], P(('dp', 'expert')), may hold values from -0.06 to 0.06
- router_weight: bfloat16 [2880, 16], replicated, may hold values from -0.109375 to 0.109375
- router_bias: float32 [16], replicated, may hold values from -4 to 4
- mlp_gain: float32 [2880], replicated, may hold values from 0.1 to 1.9
Outputs:
- dispatched: bfloat16 [16, 16, 2, 64, 2880], P('expert', None, 'dp')
- gate_slots: bfloat16 [16, 16, 2, 64], P('expert', None, 'dp')
Inputs may be any that keep to these rules, and one draw needn't show every extreme that they name: `expert_ids`: each row names 4 different experts. In each aligned block of 128 rows no expert is named more than 64 times, and one expert, the same in every block of a draw, is named exactly 64 times in every block.
All inputs are finite; a program needn't handle non-finite values.
Results may differ from a plain program's by a relative error of at most 0.012.
The roundings to bfloat16 on the way count: a program that leaves them out, or rounds other values in their place, can miss the bound.
Values may be sent and summed in bfloat16 or wider, within the bound.
A program may use at most 128 MiB of HBM per device.

v0:
```python
import functools

import jax
import jax.numpy as jnp
from jax import lax
from jax.experimental import pallas as pl
from jax.experimental.pallas import tpu as pltpu
from jax.sharding import PartitionSpec as P

HEADS = 32
KV_HEADS = 4
HEAD_DIM = 64
WINDOW = 128
MESH = pl.DeviceIdType.MESH
VMEM_BYTES = 36 * 1024 * 1024


beta_one = 0.9
beta_two = 0.999
adam_step = 100
learn_rate = 0.02
adam_eps = 1e-08
norm_eps = 1e-05
rope_base = 150000.0


def adam_weights(master, moment, second_mom, gradient):
    moment_new = beta_one * moment + (1.0 - beta_one) * gradient
    second_new = beta_two * second_mom + (1.0 - beta_two) * gradient * gradient
    fix_one = 1.0 - beta_one**adam_step
    fix_two = 1.0 - beta_two**adam_step
    update = moment_new / fix_one / (jnp.sqrt(second_new / fix_two) + adam_eps)
    return (master - learn_rate * update).astype(jnp.bfloat16)


def rotation_tables(rows):
    half_dim = HEAD_DIM // 2
    positions = jnp.arange(rows).astype(jnp.float32)
    frequency = rope_base ** (-(jnp.arange(half_dim).astype(jnp.float32) * 2.0) / HEAD_DIM)
    angles = positions[:, None] * frequency[None, :]
    cosine = jnp.cos(angles)
    sine = jnp.sin(angles)
    return (
        jnp.concatenate([cosine] * 4, axis=1),
        jnp.concatenate([-sine, sine, -sine, sine], axis=1),
    )


def chip_at(place, chips):
    place = lax.rem(place + 2 * chips, chips)
    return jnp.where(place < chips // 2, 2 * place, 2 * (chips - 1 - place) + 1)


def gather_kernel(chips, plan, top_count, *refs):
    count = len({entry[0] for entry in plan})
    if top_count:
        (source, out_ref, gate_ref, held), sems = refs[:4], refs[4:]
        ins, outs = (source,), (held,)
    else:
        ins, outs, sems = refs[:count], refs[count : 2 * count], refs[2 * count :]
    ring_send, ring_recv, pair_send, pair_recv, own_send, own_recv, own_sem = sems
    me = lax.axis_index("expert")
    core = lax.rem(me, 2)
    chip = me // 2
    place = jnp.where(lax.rem(chip, 2) == 0, chip // 2, chips - 1 - chip // 2)
    right = chip_at(place + 1, chips) * 2 + core
    left = chip_at(place - 1, chips) * 2 + core
    partner = me + 1 - 2 * core

    barrier = pltpu.get_barrier_semaphore()
    for other in (left, right, partner):
        pl.semaphore_signal(barrier, inc=1, device_id={"expert": other}, device_id_type=MESH)
    pl.semaphore_wait(barrier, 3)

    def block(j, slot):
        arr, start, size = plan[j][:3]
        return outs[arr].at[slot, pl.ds(start, size)]

    def origin(way, step):
        return chip_at(place - step if way > 0 else place + step, chips) * 2 + core

    def copy_to(j, step, send, recv, target):
        arr, start, size, way, _ = plan[j]
        slot = origin(way, step)
        return pltpu.make_async_remote_copy(
            src_ref=ins[arr].at[pl.ds(start, size)] if step == 0 else block(j, slot),
            dst_ref=block(j, slot),
            send_sem=send.at[j, step],
            recv_sem=recv.at[j, step],
            device_id={"expert": target},
            device_id_type=MESH,
        )

    def ring_copy(j, step):
        return copy_to(j, step, ring_send, ring_recv, right if plan[j][3] > 0 else left)

    def pair_copy(j, step):
        return copy_to(j, step, pair_send, pair_recv, partner)

    def own_copy(arr, slot):
        return pltpu.make_async_remote_copy(
            src_ref=ins[arr],
            dst_ref=outs[arr].at[slot],
            send_sem=own_send.at[arr],
            recv_sem=own_recv.at[arr],
            device_id={"expert": partner},
            device_id_type=MESH,
        )

    def landed(j, slot, sem):
        pltpu.make_async_copy(block(j, slot), block(j, slot), sem).wait()

    def consume(rows, slot):
        if top_count:
            fill_slots(top_count, rows, out_ref, gate_ref, slot)

    def take_mine():
        consume(ins[0], me)

    def take_partner():
        for arr in range(count):
            pltpu.make_async_copy(
                outs[arr].at[partner], outs[arr].at[partner], own_recv.at[arr]
            ).wait()
        consume(outs[0].at[partner], partner)

    def take_ring(way, step):
        slot = origin(way, step)
        consume(outs[0].at[slot], slot)

    def take_pair(ways, step):
        for j, entry in enumerate(plan):
            if entry[3] in ways and step <= entry[4]:
                landed(j, origin(entry[3], step) + 1 - 2 * core, pair_recv.at[j, step])
        slot = origin(ways[0], step) + 1 - 2 * core
        consume(outs[0].at[slot], slot)

    every = range(len(plan))
    hops = chips // 2
    for j in every:
        ring_copy(j, 0).start()
    for arr in range(count):
        own_copy(arr, me).start()
    owns = []
    if not top_count:
        owns = [
            pltpu.make_async_copy(ins[a], outs[a].at[me], own_sem.at[a]) for a in range(count)
        ]
    for copy in owns:
        copy.start()
    tasks = [take_mine, take_partner]
    for step in range(1, hops + 1):
        for j in every:
            if step > plan[j][4]:
                continue
            landed(j, origin(plan[j][3], step), ring_recv.at[j, step - 1])
            if step < plan[j][4]:
                ring_copy(j, step).start()
            pair_copy(j, step).start()
            if tasks:
                tasks.pop(0)()
        for ways in ((1,), (-1,)) if step < hops else ((1, -1),):
            tasks.append(functools.partial(take_ring, ways[0], step))
            tasks.append(functools.partial(take_pair, ways, step))
    tasks = tasks[::2] + tasks[1::2]
    for task in tasks:
        task()
    for copy in owns:
        copy.wait()
    for arr in range(count):
        own_copy(arr, me).wait_send()
    for j in every:
        for step in range(plan[j][4] + 1):
            if step:
                pair_copy(j, step).wait_send()
            if step < plan[j][4]:
                ring_copy(j, step).wait_send()


def ring_gather(arrays, cuts, sources, call_id, slots=None):
    plan = []
    chips = sources // 2
    for arr, value in enumerate(arrays):
        tiles = value.shape[0] // 16
        for cut in range(cuts):
            start = (tiles * cut + cuts - 1) // cuts * 16
            size = (tiles * (cut + 1) + cuts - 1) // cuts * 16 - start
            for way in (1, -1):
                far = (cut < cuts // 2) == (way > 0)
                plan.append((arr, start, size, way, chips // 2 - (0 if far else 1)))
    copies, count = len(plan), len(arrays)
    gathered = [jax.ShapeDtypeStruct((sources, *v.shape), v.dtype) for v in arrays]
    sems = [pltpu.SemaphoreType.DMA((copies, chips // 2 + 1))] * 4
    sems += [pltpu.SemaphoreType.DMA((count,))] * 3
    vmem = pl.BlockSpec(memory_space=pltpu.VMEM)
    if slots:
        top_count, capacity, width = slots
        out_shape = (
            jax.ShapeDtypeStruct((sources, capacity, width), jnp.bfloat16),
            jax.ShapeDtypeStruct((sources, 1, capacity), jnp.bfloat16),
        )
        out_specs = (vmem, vmem)
        held = [pltpu.VMEM(gathered[0].shape, gathered[0].dtype)]
    else:
        top_count, out_shape, held = 0, gathered, []
        out_specs = [vmem] * count
    return pl.pallas_call(
        functools.partial(gather_kernel, chips, tuple(plan), top_count),
        out_shape=out_shape,
        in_specs=[vmem] * count,
        out_specs=out_specs,
        scratch_shapes=held + sems,
        compiler_params=pltpu.CompilerParams(
            collective_id=call_id, has_side_effects=True,
            vmem_limit_bytes=(40 if slots else 24) * 1024 * 1024,
        ),
        name="ring_slots" if slots else "ring_gather",
    )(*arrays)


def ring_fits(arrays, sources):
    return sources % 4 == 0 and 8 <= sources <= 32 and all(a.shape[0] % 16 == 0 for a in arrays)


def gather_rows(arrays, sources, call_id):
    if ring_fits(arrays, sources):
        width = arrays[0].shape[1]
        return [v.reshape(-1, width) for v in ring_gather(arrays, 2, sources, call_id)]
    return [lax.all_gather(a, "expert", axis=0, tiled=True) for a in arrays]


def swap_halves(values, lane):
    up = pltpu.roll(values, 128 - HEAD_DIM // 2, 1)
    down = pltpu.roll(values, HEAD_DIM // 2, 1)
    return jnp.where(lane % HEAD_DIM < HEAD_DIM // 2, up, down)


def attention_kernel(
    heads, kv_heads, tok_ref, gain_ref, w_ref, o_ref, cos_ref, sin_ref, seg_col, seg_row, sink_ref,
    out_ref, proj_ref, att_ref,
):
    rows = tok_ref.shape[0]
    bf16 = jnp.bfloat16
    values = tok_ref[...].astype(jnp.float32)
    mean_sq = jnp.mean(values * values, axis=-1, keepdims=True)
    normed = (values * lax.rsqrt(mean_sq + norm_eps) * gain_ref[...][None, :]).astype(bf16)
    features = w_ref.shape[0]
    for start in range(0, features, 256):
        size = min(256, features - start)
        proj_ref[:, start : start + size] = lax.dot_general(
            normed, w_ref[start : start + size, :], (((1,), (1,)), ((), ())),
            preferred_element_type=jnp.float32,
        )
    lane = lax.broadcasted_iota(jnp.int32, (rows, 128), 1)
    low = lane < HEAD_DIM
    cosine, sine = cos_ref[...], sin_ref[...]
    row = lax.broadcasted_iota(jnp.int32, (rows, rows), 0)
    col = lax.broadcasted_iota(jnp.int32, (rows, rows), 1)
    offset = row - col
    allowed = (seg_col[...] == seg_row[...]) & (offset >= 0) & (offset < WINDOW)
    q_rows = heads * HEAD_DIM
    kv_rows = kv_heads * HEAD_DIM
    repeat = heads // kv_heads
    zero = jnp.zeros((rows, 128), jnp.float32)
    for group in range(kv_heads):
        base = q_rows + group // 2 * 128
        keys = proj_ref[:, base : base + 128]
        keys = keys * cosine + swap_halves(keys, lane) * sine
        vals = proj_ref[:, base + kv_rows : base + kv_rows + 128]
        keys_turned, vals_turned = pltpu.roll(keys, HEAD_DIM, 1), pltpu.roll(vals, HEAD_DIM, 1)
        if group % 2 == 1:
            keys, keys_turned, vals, vals_turned = keys_turned, keys, vals_turned, vals
        sides = (
            (jnp.where(low, keys, zero).astype(bf16), jnp.where(low, vals, zero).astype(bf16)),
            (
                jnp.where(low, zero, keys_turned).astype(bf16),
                jnp.where(low, zero, vals_turned).astype(bf16),
            ),
        )
        for slab in range(group * repeat // 2, (group + 1) * repeat // 2):
            query = proj_ref[:, slab * 128 : slab * 128 + 128]
            query = (query * cosine + swap_halves(query, lane) * sine).astype(bf16)
            total = None
            for side, (key_side, val_side) in enumerate(sides):
                scores = lax.dot_general(
                    query, key_side, (((1,), (1,)), ((), ())), preferred_element_type=jnp.float32
                ) * (HEAD_DIM**-0.5)
                weights = jnp.where(allowed, jnp.exp(scores), 0.0)
                running = jnp.exp(jnp.full((rows, 1), sink_ref[2 * slab + side])) + jnp.sum(weights, axis=-1, keepdims=True)
                probs = (weights * (1.0 / running)).astype(bf16)
                part = jnp.dot(probs, val_side, preferred_element_type=jnp.float32)
                total = part if total is None else total + part
            att_ref[:, slab * 128 : slab * 128 + 128] = total.astype(bf16)
    width = o_ref.shape[1]
    for start in range(0, width, 384):
        size = min(384, width - start)
        out_ref[:, start : start + size] = jnp.dot(
            att_ref[...], o_ref[:, start : start + size], preferred_element_type=jnp.float32
        ).astype(bf16)


def attention_call(tokens, gain, qkv_full, o_full, segments, sinks, heads, kv_heads):
    rows, width = tokens.shape
    cosine, sine = rotation_tables(rows)
    vmem = pl.BlockSpec(memory_space=pltpu.VMEM)
    return pl.pallas_call(
        functools.partial(attention_kernel, heads, kv_heads),
        out_shape=jax.ShapeDtypeStruct((rows, width), jnp.bfloat16),
        in_specs=[vmem] * 8 + [pl.BlockSpec(memory_space=pltpu.SMEM)],
        out_specs=vmem,
        scratch_shapes=[
            pltpu.VMEM((rows, qkv_full.shape[0]), jnp.float32),
            pltpu.VMEM((rows, heads * HEAD_DIM), jnp.bfloat16),
        ],
        compiler_params=pltpu.CompilerParams(vmem_limit_bytes=VMEM_BYTES),
        name="attention_part",
    )(
        tokens, gain, qkv_full, o_full, cosine, sine, segments[:, None],
        segments[None, :], sinks,
    )


def exchange_kernel(part_ref, got_ref, send_sem, recv_sem):
    group = lax.axis_index("dp")
    other = 1 - group
    barrier = pltpu.get_barrier_semaphore()
    pl.semaphore_signal(barrier, inc=1, device_id={"dp": other}, device_id_type=MESH)
    pl.semaphore_wait(barrier, 1)
    copy = pltpu.make_async_remote_copy(
        src_ref=part_ref.at[other],
        dst_ref=got_ref,
        send_sem=send_sem,
        recv_sem=recv_sem,
        device_id={"dp": other},
        device_id_type=MESH,
    )
    copy.start()
    copy.wait()


def exchange_call(part, call_id):
    return pl.pallas_call(
        exchange_kernel,
        out_shape=jax.ShapeDtypeStruct(part.shape[1:], part.dtype),
        in_specs=[pl.BlockSpec(memory_space=pltpu.VMEM)],
        out_specs=pl.BlockSpec(memory_space=pltpu.VMEM),
        scratch_shapes=[pltpu.SemaphoreType.DMA, pltpu.SemaphoreType.DMA],
        compiler_params=pltpu.CompilerParams(
            collective_id=call_id, has_side_effects=True, vmem_limit_bytes=16 * 1024 * 1024
        ),
        name="exchange_halves",
    )(part)


def router_kernel(tok_ref, part_ref, got_ref, gain_ref, rw_ref, bias_ref, ids_ref, out_ref):
    group = lax.axis_index("dp")
    half, width = got_ref.shape
    experts = rw_ref.shape[0]
    top_count = ids_ref.shape[1]
    rows = pl.ds(pl.multiple_of(group * half, half), half)
    summed = part_ref[group].astype(jnp.float32) + got_ref[...].astype(jnp.float32)
    residual = tok_ref[rows, :].astype(jnp.float32) + summed
    mean_sq = jnp.mean(residual * residual, axis=-1, keepdims=True)
    moe_in = (residual * lax.rsqrt(mean_sq + norm_eps) * gain_ref[...][None, :]).astype(jnp.bfloat16)
    out_ref[:, :width] = moe_in
    logits = lax.dot_general(
        moe_in, rw_ref[...], (((1,), (1,)), ((), ())), preferred_element_type=jnp.float32
    ) + bias_ref[...]
    ids = ids_ref[rows, :]
    expert = lax.broadcasted_iota(jnp.int32, (half, experts), 1)
    picked = [ids[:, k : k + 1] == expert for k in range(top_count)]
    hit = sum(jnp.where(p, 1.0, 0.0) for p in picked)
    above = lax.broadcasted_iota(jnp.int32, (half, half), 0) > lax.broadcasted_iota(
        jnp.int32, (half, half), 1
    )
    before = jnp.dot(
        jnp.where(above, 1.0, 0.0).astype(jnp.bfloat16), hit.astype(jnp.bfloat16),
        preferred_element_type=jnp.float32,
    )
    raised = [jnp.exp(jnp.sum(jnp.where(p, logits, 0.0), axis=1, keepdims=True)) for p in picked]
    scale = 1.0 / sum(raised)
    column = lax.broadcasted_iota(jnp.int32, (half, out_ref.shape[1] - width), 1)
    extra = jnp.zeros(column.shape, jnp.float32)
    for k in range(top_count):
        slot = jnp.sum(jnp.where(picked[k], before, 0.0), axis=1, keepdims=True)
        extra = jnp.where(column == 3 * k, raised[k] * scale, extra)
        extra = jnp.where(column == 3 * k + 1, ids[:, k : k + 1].astype(jnp.float32), extra)
        extra = jnp.where(column == 3 * k + 2, slot, extra)
    out_ref[:, width:] = extra.astype(jnp.bfloat16)


def router_call(tokens, part, got, gain, router_weight, router_bias, expert_ids, extra):
    half, width = got.shape
    return pl.pallas_call(
        router_kernel,
        out_shape=jax.ShapeDtypeStruct((half, width + extra), jnp.bfloat16),
        in_specs=[pl.BlockSpec(memory_space=pltpu.VMEM)] * 7,
        out_specs=pl.BlockSpec(memory_space=pltpu.VMEM),
        compiler_params=pltpu.CompilerParams(vmem_limit_bytes=VMEM_BYTES),
        name="router_part",
    )(tokens, part, got, gain, router_weight.T, router_bias[None, :], expert_ids)


def fill_slots(top_count, rows_ref, out_ref, gate_ref, slot):
    mine = lax.axis_index("expert").astype(jnp.float32)
    _, capacity, width = out_ref.shape
    half, full = rows_ref.shape
    extra = rows_ref[:, full - 128 :].astype(jnp.float32)
    shift = 128 - (full - width)
    place = lax.broadcasted_iota(jnp.int32, (half, capacity), 1).astype(jnp.float32)
    select = jnp.zeros((half, capacity), jnp.float32)
    gates = jnp.zeros((half, capacity), jnp.float32)
    for k in range(top_count):
        at = shift + 3 * k
        match = (extra[:, at + 1 : at + 2] == mine) & (extra[:, at + 2 : at + 3] == place)
        select = jnp.where(match, 1.0, select)
        gates = jnp.where(match, extra[:, at : at + 1], gates)
    gate_ref[slot] = jnp.sum(gates, axis=0, keepdims=True).astype(jnp.bfloat16)
    out_ref[slot] = lax.dot_general(
        select.astype(jnp.bfloat16), rows_ref[:, :width], (((0,), (0,)), ((), ())),
        preferred_element_type=jnp.float32,
    ).astype(jnp.bfloat16)


def exchange_slots(rows, width, experts, capacity, top_count, sources):
    half = rows.shape[0]
    extra = rows[:, width:].astype(jnp.float32)
    moe_in = rows[:, :width]
    gates, ids, slots = (extra[:, i : 3 * top_count : 3] for i in range(3))
    target = (ids * capacity + slots).astype(jnp.int32).reshape(-1)
    matches = target[None, :] == jnp.arange(experts * capacity, dtype=jnp.int32)[:, None]
    token_match = jnp.any(matches.reshape(experts * capacity, half, top_count), axis=2)
    payload = jnp.dot(
        token_match.astype(jnp.bfloat16), moe_in, preferred_element_type=jnp.float32
    ).astype(jnp.bfloat16)
    slot_gates = jnp.sum(jnp.where(matches, gates.reshape(-1)[None, :], 0.0), axis=1)
    outgoing = (
        payload.reshape(experts, capacity, width),
        slot_gates.astype(jnp.bfloat16).reshape(experts, capacity),
    )
    got_rows, got_gates = (
        lax.all_to_all(v, "expert", split_axis=0, concat_axis=0, tiled=True) for v in outgoing
    )
    per_device = experts // sources
    got_rows = got_rows.reshape(sources, per_device, capacity, width)
    got_gates = got_gates.reshape(sources, per_device, capacity)
    return (
        jnp.transpose(got_rows, (1, 0, 2, 3))[:, :, None],
        jnp.transpose(got_gates, (1, 0, 2))[:, :, None],
    )


def on_device(
    tokens,
    segment_ids,
    expert_ids,
    attn_gain,
    sinks,
    qkv_master,
    qkv_mom,
    qkv_var,
    qkv_grad,
    o_master,
    o_mom,
    o_var,
    o_grad,
    router_weight,
    router_bias,
    mlp_gain,
):
    tok_rows, width = tokens.shape
    half = tok_rows // lax.axis_size("dp")
    sources = lax.axis_size("expert")
    heads_here = sinks.shape[0]
    kv_here = KV_HEADS * heads_here // HEADS
    experts = router_weight.shape[1]
    top_count = expert_ids.shape[1]
    capacity = 2 * half * top_count // experts
    qkv_local = adam_weights(qkv_master, qkv_mom, qkv_var, qkv_grad)
    o_local = adam_weights(o_master, o_mom, o_var, o_grad)
    qkv_full, o_full = gather_rows([qkv_local, o_local], sources, 1)
    part = attention_call(
        tokens, attn_gain, qkv_full, o_full, segment_ids, sinks, heads_here, kv_here
    ).reshape(-1, half, width)
    got = exchange_call(part, 2)
    rows = router_call(
        tokens, part, got, mlp_gain, router_weight, router_bias, expert_ids, 128 - width % 128
    )
    compact = sources * half <= 2 * experts * capacity
    if experts == sources and compact and ring_fits([rows], sources):
        dispatched, gate_slots = ring_gather(
            [rows], 4, sources, 3, (top_count, capacity, width)
        )
        return (dispatched[None, :, None], gate_slots[None])
    return exchange_slots(rows, width, experts, capacity, top_count, sources)


def solution(mesh):
    return jax.shard_map(
        on_device,
        mesh=mesh,
        in_specs=(
            P("expert", None),
            P("expert"),
            P("expert", None),
            P(),
            P("dp"),
            P(("dp", "expert"), None),
            P(("dp", "expert"), None),
            P(("dp", "expert"), None),
            P(("dp", "expert"), None),
            P(("dp", "expert"), None),
            P(("dp", "expert"), None),
            P(("dp", "expert"), None),
            P(("dp", "expert"), None),
            P(),
            P(),
            P(),
        ),
        out_specs=(P("expert", None, "dp", None, None), P("expert", None, "dp", None)),
        check_vma=False,
    )
```

profile of v0, /device:TPU:1, one launch (start us, length us, event | category | flops | bytes accessed | tf_op | source)
XLA Modules:
  0.0 190.4 jit_solution(14141415789233338602)
XLA Ops:
  0.6 0.0 copy-start.12
  0.7 0.5 fusion.16
  1.2 0.0 copy-start.9
  1.2 0.0 copy-start.8
  1.2 0.0 copy-start.10
  1.2 0.3 pad_maximum_fusion
  1.5 2.7 %fusion.7.refs_0_ = bf16[80,2880]{1,0:T(8,128)(2,1)S(1)} fusion(f32[80,2880]{1,0:T(8,128)} %param.21, f32[80,2880]{1,0:T(8,128)} %param.24, f32[80,2880]{1,0:T(8,128)} %param.23, f32[80,2880]{1,0:T(8,128)} %param.22), kind=kLoop, calls=%fused_computation.9 | loop fusion | flops 3225600 | bytes 4147200 | tf_op jit(solution)/shard_map/convert_element_type | solution.py:33
  4.2 2.3 %fusion.15.refs_1_ = bf16[64,2880]{1,0:T(8,128)(2,1)S(1)} fusion(f32[64,2880]{1,0:T(8,128)} %param.25, f32[64,2880]{1,0:T(8,128)} %param.28, f32[64,2880]{1,0:T(8,128)} %param.27, f32[64,2880]{1,0:T(8,128)} %param.26), kind=kLoop, calls=%fused_computation.17 | loop fusion | flops 2580480 | bytes 3317760 | tf_op jit(solution)/shard_map/convert_element_type | solution.py:33
  6.6 72.4 %ring_gather.1 = (bf16[16,80,2880]{2,1,0:T(8,128)(2,1)S(1)}, bf16[16,64,2880]{2,1,0:T(8,128)(2,1)S(1)}) custom-call(bf16[80,2880]{1,0:T(8,128)(2,1)S(1)} %fusion.7.refs_0_, bf16[64,2880]{1,0:T(8,128)(2,1)S(1)} %fusion.15.refs_1_), custom_call_target="tpu_custom_call" | custom-call | tf_op jit(solution)/shard_map/ring_gather/pallas_call | solution.py:207
  79.0 0.0 copy-start
  79.0 3.0 %copy-done = bf16[16,80,2880]{2,1,0:T(8,128)(2,1)} copy-done((bf16[16,80,2880]{2,1,0:T(8,128)(2,1)}, bf16[16,80,2880]{2,1,0:T(8,128)(2,1)S(1)}, u32[]{:S(2)}) %copy-start) | copy-done | bytes 7372824
  82.0 0.0 copy-start.2
  82.0 2.6 %copy-done.2 = bf16[16,64,2880]{2,1,0:T(8,128)(2,1)} copy-done((bf16[16,64,2880]{2,1,0:T(8,128)(2,1)}, bf16[16,64,2880]{2,1,0:T(8,128)(2,1)S(1)}, u32[]{:S(2)}) %copy-start.2) | copy-done | bytes 5898264
  84.6 0.0 copy-done.12
  84.6 1.2 copy.30.tok_ref
  85.8 0.0 copy-done.9
  85.8 0.1 copy.29.seg_col
  85.9 0.0 copy-done.8
  85.9 0.0 copy-done.10
  85.9 0.0 copy-start.1
  86.0 3.1 %copy-done.1 = bf16[16,80,2880]{2,1,0:T(8,128)(2,1)S(1)} copy-done((bf16[16,80,2880]{2,1,0:T(8,128)(2,1)S(1)}, bf16[16,80,2880]{2,1,0:T(8,128)(2,1)}, u32[]{:S(2)}) %copy-start.1) | copy-done | bytes 7372824
  89.1 0.0 copy-start.3
  89.1 2.7 %copy-done.3 = bf16[16,64,2880]{2,1,0:T(8,128)(2,1)S(1)} copy-done((bf16[16,64,2880]{2,1,0:T(8,128)(2,1)S(1)}, bf16[16,64,2880]{2,1,0:T(8,128)(2,1)}, u32[]{:S(2)}) %copy-start.3) | copy-done | bytes 5898264
  91.8 0.0 copy-start.13
  91.8 0.0 copy-start.6
  91.8 0.0 copy-start.7
  91.8 0.0 copy-start.11
  91.8 8.9 %attention_part.1 = bf16[256,2880]{1,0:T(8,128)(2,1)S(1)} custom-call(bf16[256,2880]{1,0:T(8,128)(2,1)S(1)} %copy.30.tok_ref, f32[2880]{0:T(1024)S(1)} %copy-done.8, bf16[1280,2880]{1,0:T(8,128)(2,1)S(1)} %bitcast.15, bf16[1024,2880]{1,0:T(8,128)(2,1)S(1)} %bitcast.17, f32[256,128]{1,0:T(8,128)S(1)} %get-tuple-element.19.cos_ref, ...), custom_call_target="tpu_custom_call" | custom-call | tf_op jit(solution)/shard_map/attention_part/pallas_call | solution.py:306
  100.7 18.4 %exchange_halves.1.got_ref = bf16[128,2880]{1,0:T(8,128)(2,1)S(1)} custom-call(bf16[2,128,2880]{2,1,0:T(8,128)(2,1)S(1)} %bitcast.13), custom_call_target="tpu_custom_call" | custom-call | tf_op jit(solution)/shard_map/exchange_halves/pallas_call | solution.py:342
  119.1 0.0 copy-start.4
  119.1 0.9 copy-done.4
  120.0 0.0 copy-done.13
  120.0 0.1 copy.31.ids_ref
  120.1 0.0 copy-done.6
  120.1 0.0 copy-done.7
  120.1 0.0 copy-done.11
  120.2 0.0 copy-start.5
  120.2 1.1 copy-done.5
  121.3 1.1 router_part.1.refs_0_
  122.4 64.8 %ring_slots.1 = (bf16[16,64,2880]{2,1,0:T(8,128)(2,1)S(1)}, bf16[16,1,64]{2,1,0:T(2,128)(2,1)S(1)}) custom-call(bf16[128,2944]{1,0:T(8,128)(2,1)S(1)} %router_part.1.refs_0_), custom_call_target="tpu_custom_call" | custom-call | tf_op jit(solution)/shard_map/ring_slots/pallas_call | solution.py:207
  187.2 0.6 copy.35
  187.8 2.6 %copy.37 = bf16[1,16,1,64,2880]{4,3,2,1,0:T(8,128)(2,1)} copy(bf16[1,16,1,64,2880]{4,3,2,1,0:T(8,128)(2,1)S(1)} %bitcast.16) | data formatting | bytes 11796480
  (2 shorter events, 0.0 us)
Async XLA Ops:
  0.6 84.0 %copy-start.12 = (bf16[256,2880]{0,1:T(8,128)(2,1)S(1)}, bf16[256,2880]{0,1:T(8,128)(2,1)}, u32[]{:S(2)}) copy-start(bf16[256,2880]{0,1:T(8,128)(2,1)} %param.16) | copy-start | bytes 4423684
  1.2 84.6 %copy-start.9 = (s32[256]{0:T(256)S(1)}, s32[256]{0:T(256)}, u32[]{:S(2)}) copy-start(s32[256]{0:T(256)} %param.17) | copy-start | bytes 3076
  1.2 84.7 %copy-start.8 = (f32[2880]{0:T(1024)S(1)}, f32[2880]{0:T(1024)}, u32[]{:S(2)}) copy-start(f32[2880]{0:T(1024)} %gain_ref.2) | copy-start | bytes 34564
  1.2 84.7 %copy-start.10 = (f32[16]{0:T(128)S(1)}, f32[16]{0:T(128)}, u32[]{:S(2)}) copy-start(f32[16]{0:T(128)} %sink_ref.1) | copy-start | bytes 196
  79.0 3.0 %copy-start = (bf16[16,80,2880]{2,1,0:T(8,128)(2,1)}, bf16[16,80,2880]{2,1,0:T(8,128)(2,1)S(1)}, u32[]{:S(2)}) copy-start(bf16[16,80,2880]{2,1,0:T(8,128)(2,1)S(1)} %get-tuple-element.6) | copy-start | bytes 22118404
  82.0 2.6 %copy-start.2 = (bf16[16,64,2880]{2,1,0:T(8,128)(2,1)}, bf16[16,64,2880]{2,1,0:T(8,128)(2,1)S(1)}, u32[]{:S(2)}) copy-start(bf16[16,64,2880]{2,1,0:T(8,128)(2,1)S(1)} %get-tuple-element.7) | copy-start | bytes 17694724
  85.9 3.1 %copy-start.1 = (bf16[16,80,2880]{2,1,0:T(8,128)(2,1)S(1)}, bf16[16,80,2880]{2,1,0:T(8,128)(2,1)}, u32[]{:S(2)}) copy-start(bf16[16,80,2880]{2,1,0:T(8,128)(2,1)} %copy-done) | copy-start | bytes 22118404
  89.1 2.7 %copy-start.3 = (bf16[16,64,2880]{2,1,0:T(8,128)(2,1)S(1)}, bf16[16,64,2880]{2,1,0:T(8,128)(2,1)}, u32[]{:S(2)}) copy-start(bf16[16,64,2880]{2,1,0:T(8,128)(2,1)} %copy-done.2) | copy-start | bytes 17694724
  91.8 28.2 %copy-start.13 = (s32[256,4]{0,1:T(4,128)S(1)}, s32[256,4]{0,1:T(4,128)}, u32[]{:S(2)}) copy-start(s32[256,4]{0,1:T(4,128)} %param.18) | copy-start | bytes 12292
  91.8 28.3 %copy-start.6 = (bf16[2880,16]{0,1:T(8,128)(2,1)S(1)}, bf16[2880,16]{0,1:T(8,128)(2,1)}, u32[]{:S(2)}) copy-start(bf16[2880,16]{0,1:T(8,128)(2,1)} %param.29) | copy-start | bytes 276484
  91.8 28.3 %copy-start.7 = (f32[2880]{0:T(1024)S(1)}, f32[2880]{0:T(1024)}, u32[]{:S(2)}) copy-start(f32[2880]{0:T(1024)} %gain_ref.3) | copy-start | bytes 34564
  91.8 28.3 %copy-start.11 = (f32[16]{0:T(128)S(1)}, f32[16]{0:T(128)}, u32[]{:S(2)}) copy-start(f32[16]{0:T(128)} %param.30) | copy-start | bytes 196
  119.1 0.9 copy-start.4
  120.2 1.1 copy-start.5
where the time goes:
time: 191 us; the launch traced here: 190 us
  Pallas kernels  166 us (87%)
  local copies, waits for them, and re-layouts  18.1 us (9%)
  other arithmetic  5.87 us (3%)
    pallas_call x2, Pallas kernels, ring_gather(): pl.pallas_call(functools.partial(gather_kernel, chips, tuple(plan), top_c...  137 us
    pallas_call x1, Pallas kernels, exchange_call(): pl.pallas_call(exchange_kernel, out_shape=jax.ShapeDtypeStruct(part.shape...  18.4 us
    unnamed x32, local copies, waits for them, and re-layouts  18 us
    pallas_call x1, Pallas kernels, attention_call(): pl.pallas_call(functools.partial(attention_kernel, heads, kv_heads), out_...  8.88 us
    convert_element_type x2, other arithmetic, adam_weights(): return (master - learn_rate * update).astype(jnp.bfloat16)  5.05 us

commit v1 on v0

--- a/solution.py
+++ b/solution.py
@@ -1,7 +1,9 @@
 import functools
+import types
 
 import jax
 import jax.numpy as jnp
+import numpy as np
 from jax import lax
 from jax.experimental import pallas as pl
 from jax.experimental.pallas import tpu as pltpu
@@ -450,6 +452,594 @@
     )
 
 
+def split_tables(rows):
+    half_dim = HEAD_DIM // 2
+    positions = np.arange(rows).astype(np.float64)
+    powers = -(np.arange(half_dim).astype(np.float64) * 2.0) / HEAD_DIM
+    frequency = (rope_base**powers).astype(np.float32).astype(np.float64)
+    angles = (positions[:, None] * frequency[None, :]).astype(np.float32).astype(np.float64)
+    cosine, sine = np.cos(angles), np.sin(angles)
+    return (
+        np.concatenate([cosine] * 4, axis=1).astype(np.float32),
+        np.concatenate([-sine, sine, -sine, sine], axis=1).astype(np.float32),
+    )
+
+
+def piece_plan(groups, hops):
+    plan, base = [], 0
+    for group, spans in enumerate(groups):
+        for start, size, far_way in spans:
+            for way in (1, -1):
+                count = hops if way == far_way else hops - 1
+                plan.append((group, start, size, way, count, base))
+                base += count
+    return tuple(plan), base
+
+
+def layer_kernel(cfg, hbm, r):
+    bf16, f32 = jnp.bfloat16, jnp.float32
+    chips, plan = cfg.chips, cfg.plan
+    hops = chips // 2
+    me = lax.axis_index("expert")
+    side = lax.axis_index("dp")
+    core = lax.rem(me, 2)
+    chip = me // 2
+    place = jnp.where(lax.rem(chip, 2) == 0, chip // 2, chips - 1 - chip // 2)
+    right = chip_at(place + 1, chips) * 2 + core
+    left = chip_at(place - 1, chips) * 2 + core
+    flip = 1 - 2 * core
+    partner = me + flip
+    across = 1 - side
+    rows, width = r.tok.shape
+    half = rows // 2
+    q_block = r.q_in.shape[1]
+    o_block = r.o_in.shape[1]
+    capacity = r.out.shape[1]
+    cut = cfg.segments[0][1]
+
+    names = []
+
+    def load(name, pairs):
+        for src, dst in pairs:
+            pltpu.make_async_copy(src, dst, r.load_sem.at[len(names)]).start()
+        names.append(name)
+
+    def ready(name, ref):
+        pltpu.make_async_copy(ref, ref, r.load_sem.at[names.index(name)]).wait()
+
+    def tile_of(start):
+        return r.q_in.at[:, pl.ds(start, 16)]
+
+    for start in range(0, q_block, 16):
+        part = pl.ds(start, 16)
+        load(start, [(hbm.adam[i].at[part], r.q_in.at[i, part]) for i in range(4)])
+    load("tok", [(hbm.tok, r.tok_t)])
+    load("o", [(hbm.adam[4 + i], r.o_in.at[i]) for i in range(4)])
+    for index, pair in enumerate(zip(hbm.small, r.small)):
+        load(-1 - index, [pair])
+    gain, mlp, seg_row, cosine, sine, router, bias, ids_ref, sinks = r.small
+
+    barrier = pltpu.get_barrier_semaphore()
+    for other in (left, right, partner):
+        pl.semaphore_signal(barrier, inc=1, device_id={"expert": other}, device_id_type=MESH)
+    pl.semaphore_signal(barrier, inc=1, device_id={"dp": across}, device_id_type=MESH)
+    pl.semaphore_wait(barrier, 4)
+
+    swaps = len(cfg.segments)
+    fast, slow, marks = swaps + 2, swaps + 3, swaps + 4
+    full = width // 128 * 128
+    held = (r.w_q, r.tails, *r.o_part, r.rows_a, r.rows_b, r.notes)
+    stride = (q_block, 0, *[o_block] * swaps, 0, 0, 0)
+
+    def block(group, slot, start, size):
+        ref = held[group]
+        columns = pl.ds(0, ref.shape[-1] // 128 * 128)
+        if stride[group]:
+            first = pl.multiple_of(slot * stride[group] + start, 16)
+            return ref.at[pl.ds(first, size), columns]
+        return ref.at[slot, pl.ds(start, size), columns]
+
+    def blocks(group, count):
+        if stride[group]:
+            return block(group, 0, 0, count * stride[group])
+        columns = pl.ds(0, held[group].shape[-1] // 128 * 128)
+        return held[group].at[pl.ds(0, count), :, columns]
+
+    def origin(way, step):
+        return chip_at(place - step if way > 0 else place + step, chips) * 2 + core
+
+    def send(ref, device, out_sem, in_sem):
+        return pltpu.make_async_remote_copy(
+            src_ref=ref, dst_ref=ref, send_sem=out_sem, recv_sem=in_sem,
+            device_id={"expert": device}, device_id_type=MESH,
+        )
+
+    def ring_copy(entry, step):
+        group, start, size, way, _, base = entry
+        return send(
+            block(group, origin(way, step), start, size), right if way > 0 else left,
+            r.ring_send.at[group], r.ring_recv.at[base + step],
+        )
+
+    def mark(group, way, step):
+        if group < fast:
+            return group
+        at = fast + 2 * hops * (group - fast)
+        return at if step == 0 else at + (2 * step - (way > 0) if step < hops else 2 * step - 1)
+
+    def pair_copy(entry, step):
+        group, start, size, way, _, _ = entry
+        return send(
+            block(group, origin(way, step), start, size), partner,
+            r.pair_send.at[group], r.pair_recv.at[mark(group, way, step)],
+        )
+
+    def own_copy(group):
+        return send(
+            block(group, me, 0, cfg.own[group]), partner, r.pair_send.at[group],
+            r.pair_recv.at[mark(group, 1, 0)],
+        )
+
+    def landed(ref, sem):
+        pltpu.make_async_copy(ref, ref, sem).wait()
+
+    def entries(group, step):
+        return [e for e in plan if e[0] == group and e[4] >= step]
+
+    tasks = []
+
+    def own_sends(group, starts=None, last=True):
+        for entry in entries(group, 0):
+            if starts is None or entry[1] in starts:
+                ring_copy(entry, 0).start()
+        if last:
+            own_copy(group).start()
+
+    def advance(group, step, starts=None):
+        for entry in entries(group, step):
+            _, start, size, way, far, base = entry
+            if starts is not None and start not in starts:
+                continue
+            landed(block(group, origin(way, step), start, size), r.ring_recv.at[base + step - 1])
+            if step < far:
+                ring_copy(entry, step).start()
+            pair_copy(entry, step).start()
+            if tasks:
+                tasks.pop(0)()
+
+    def pair_wait(group, way, step):
+        slot = origin(way, step) + flip if step else partner
+        landed(block(group, slot, 0, cfg.own[group]), r.pair_recv.at[mark(group, way, step)])
+
+    def all_here(group):
+        landed(blocks(group, chips), r.pair_recv.at[group])
+
+    def adam_part(ref, part, columns):
+        return adam_weights(*(ref[i, part, columns] for i in range(4)))
+
+    upper = cfg.tops[0]
+
+    def adam_qkv(start):
+        ready(start, tile_of(start))
+        part = pl.ds(pl.multiple_of(me * q_block + start, 16), 16)
+        fresh = adam_part(r.q_in, slice(start, start + 16), slice(None))
+        r.w_q[part, :] = fresh
+        at, lanes = (start, 0) if start < upper else (start - upper, 64)
+        r.tails[me, at : at + 16, lanes : lanes + 64] = fresh[:, full:]
+
+    starts = list(range(0, q_block, 16))
+    for index, start in enumerate(starts):
+        adam_qkv(start)
+        if index:
+            own_sends(0, starts[index - 1 : index], False)
+    ready("o", r.o_in)
+    first = pl.multiple_of(me * o_block, 16)
+    for part, (start, size) in zip(r.o_part, cfg.segments):
+        fresh = adam_part(r.o_in, slice(None), slice(start, start + size))
+        part[pl.ds(first, o_block), :] = fresh
+    lower = o_block // 2
+    r.tails[me, upper:, :64] = fresh[:lower, size - 64 :]
+    r.tails[me, upper:, 64:] = fresh[lower:, size - 64 :]
+    own_sends(0, starts[-1:])
+    own_sends(1)
+    ready("tok", r.tok_t)
+    for start in range(0, width, 128):
+        part = r.tok_t[start : min(start + 128, width), :].astype(f32)
+        r.tok[:, start : min(start + 128, width)] = jnp.transpose(part).astype(bf16)
+    ready(-1, gain)
+    values = r.tok[...].astype(f32)
+    mean_sq = jnp.mean(values * values, axis=-1, keepdims=True)
+    r.normed[...] = (
+        values * lax.rsqrt(mean_sq + norm_eps) * gain[...][None, :]
+    ).astype(bf16)
+    for index, ref in enumerate(r.small[1:]):
+        ready(-2 - index, ref)
+    row = lax.broadcasted_iota(jnp.int32, (rows, rows), 0)
+    col = lax.broadcasted_iota(jnp.int32, (rows, rows), 1)
+    offset = row - col
+    across_row = seg_row[...].astype(f32)
+    down = jnp.transpose(jnp.broadcast_to(across_row, (128, rows)))
+    down = jnp.concatenate([down] * (rows // 128), axis=1)
+    allowed = (down == across_row) & (offset >= 0) & (offset < WINDOW)
+    r.mask[...] = jnp.where(allowed, 1.0, 0.0)
+
+    def project(start):
+        size = min(256, r.w_q.shape[0] - start)
+        r.proj[:, start : start + size] = lax.dot_general(
+            r.normed[...], r.w_q[start : start + size, :], (((1,), (1,)), ((), ())),
+            preferred_element_type=f32,
+        )
+
+    lane = lax.broadcasted_iota(jnp.int32, (rows, 128), 1)
+    low = lane < HEAD_DIM
+    q_rows = cfg.heads * HEAD_DIM
+    kv_rows = cfg.kv_heads * HEAD_DIM
+    repeat = cfg.heads // cfg.kv_heads
+    kept = {}
+
+    def attend(slab):
+        allowed = r.mask[...] > 0.0
+        zero = jnp.zeros((rows, 128), f32)
+        group = slab * 2 // repeat
+        if group not in kept:
+            base = q_rows + group // 2 * 128
+            keys = r.proj[:, base : base + 128]
+            keys = keys * cosine[...] + swap_halves(keys, lane) * sine[...]
+            vals = r.proj[:, base + kv_rows : base + kv_rows + 128]
+            keys_turned, vals_turned = pltpu.roll(keys, HEAD_DIM, 1), pltpu.roll(vals, HEAD_DIM, 1)
+            if group % 2 == 1:
+                keys, keys_turned, vals, vals_turned = keys_turned, keys, vals_turned, vals
+            kept[group] = (
+                (jnp.where(low, keys, zero).astype(bf16), jnp.where(low, vals, zero).astype(bf16)),
+                (
+                    jnp.where(low, zero, keys_turned).astype(bf16),
+                    jnp.where(low, zero, vals_turned).astype(bf16),
+                ),
+            )
+        query = r.proj[:, slab * 128 : slab * 128 + 128]
+        query = (query * cosine[...] + swap_halves(query, lane) * sine[...]).astype(bf16)
+        total = None
+        for which, (key_side, val_side) in enumerate(kept[group]):
+            scores = lax.dot_general(
+                query, key_side, (((1,), (1,)), ((), ())), preferred_element_type=f32
+            ) * (HEAD_DIM**-0.5)
+            weights = jnp.where(allowed, jnp.exp(scores), 0.0)
+            sink = jnp.exp(jnp.full((rows, 1), sinks[2 * slab + which]))
+            running = sink + jnp.sum(weights, axis=-1, keepdims=True)
+            probs = (weights * (1.0 / running)).astype(bf16)
+            part = jnp.dot(probs, val_side, preferred_element_type=f32)
+            total = part if total is None else total + part
+        r.att[:, slab * 128 : slab * 128 + 128] = total.astype(bf16)
+
+    ours = pl.ds(pl.multiple_of(side * half, half), half)
+    theirs = pl.ds(pl.multiple_of(across * half, half), half)
+
+    def swap_copy(index):
+        return pltpu.make_async_remote_copy(
+            src_ref=r.swap_out[index], dst_ref=r.swap_in[index],
+            send_sem=r.swap_send.at[index], recv_sem=r.swap_recv.at[index],
+            device_id={"dp": across}, device_id_type=MESH,
+        )
+
+    def product(index, which):
+        start, size = cfg.segments[index]
+        for at in range(0, size, 512):
+            span = min(512, size - at)
+            part = jnp.dot(
+                r.att[ours if which else theirs, :], r.o_part[index][:, at : at + span],
+                preferred_element_type=f32,
+            )
+            if which:
+                total = r.tok[ours, start + at : start + at + span].astype(f32) + part
+                r.res[:, start + at : start + at + span] = total
+            else:
+                r.swap_out[index][:, at : at + span] = part.astype(bf16)
+
+    def swap(index):
+        product(index, 0)
+        swap_copy(index).start()
+        product(index, 1)
+
+    def receive(index):
+        start, size = cfg.segments[index]
+        landed(r.swap_in[index], r.swap_recv.at[index])
+        r.res[:, start : start + size] += r.swap_in[index][...].astype(f32)
+
+    heads_slabs = cfg.heads // 2
+    spans = range(0, r.w_q.shape[0], 256)
+
+    def unpack_tails():
+        part = r.o_part[-1]
+        edge = part.shape[1] - 64
+        for slot in range(2 * chips):
+            low_half, high_half = slice(0, 64), slice(64, 128)
+            at = slot * q_block
+            r.w_q[at : at + upper, full:] = r.tails[slot, :upper, low_half]
+            r.w_q[at + upper : at + q_block, full:] = r.tails[slot, : q_block - upper, high_half]
+            at = slot * o_block
+            part[at : at + lower, edge:] = r.tails[slot, upper:, low_half]
+            part[at + lower : at + o_block, edge:] = r.tails[slot, upper:, high_half]
+
+    advance(0, 1)
+    advance(1, 1)
+    own_sends(2)
+    for step in range(2, hops):
+        advance(0, step)
+        advance(1, step)
+        advance(2, step - 1)
+    own_sends(3)
+    advance(0, hops)
+    advance(1, hops)
+    all_here(0)
+    all_here(1)
+    unpack_tails()
+    for start in spans[:3]:
+        project(start)
+    advance(2, hops - 1)
+    own_sends(4)
+    for start in spans[3:]:
+        project(start)
+    for slab in range(heads_slabs // 2):
+        attend(slab)
+    advance(3, 1)
+    for slab in range(heads_slabs // 2, heads_slabs):
+        attend(slab)
+    advance(2, hops)
+    all_here(2)
+    swap(0)
+    advance(4, 1)
+    advance(3, 2)
+    advance(4, 2)
+    advance(3, 3)
+    receive(0)
+    r.rows_a[me] = r.res[:, :cut].astype(bf16)
+    early, late = (0, half // 4), (half // 2, 3 * half // 4)
+    own_sends(fast, early, False)
+    advance(4, 3)
+    own_sends(fast, late)
+    advance(3, 4)
+    all_here(3)
+    swap(1)
+    advance(fast, 1, early)
+    advance(4, 4)
+    all_here(4)
+    swap(2)
+    advance(fast, 1, late)
+    receive(1)
+    advance(fast, 2)
+    receive(2)
+
+    experts = router.shape[0]
+    top_count = cfg.top_count
+    residual = r.res[...]
+    mean_sq = jnp.mean(residual * residual, axis=-1, keepdims=True)
+    scale = lax.rsqrt(mean_sq + norm_eps)
+    head = (r.res[:, :cut] * scale * mlp[:cut][None, :]).astype(bf16)
+    tail = (r.res[:, cut:] * scale * mlp[cut:][None, :]).astype(bf16)
+    r.rows_b[me] = tail
+    edge = tail.shape[1] - 64
+    quiet = r.notes.shape[1] - half // 2
+    r.notes[me, quiet:, :64] = tail[: half // 2, edge:]
+    r.notes[me, quiet:, 64:] = tail[half // 2 :, edge:]
+    across_lanes = (((1,), (1,)), ((), ()))
+    logits = (
+        lax.dot_general(router[:, :cut], head, across_lanes, preferred_element_type=f32)
+        + lax.dot_general(router[:, cut:], tail, across_lanes, preferred_element_type=f32)
+        + jnp.transpose(jnp.broadcast_to(bias[...], (half, experts)))
+    )
+    ids = ids_ref[:, ours]
+    expert = lax.broadcasted_iota(jnp.int32, (experts, half), 0)
+    picked = [ids[k : k + 1, :] == expert for k in range(top_count)]
+    hit = sum(jnp.where(p, 1.0, 0.0) for p in picked)
+    earlier = lax.broadcasted_iota(jnp.int32, (half, half), 0) < lax.broadcasted_iota(
+        jnp.int32, (half, half), 1
+    )
+    before = jnp.dot(
+        hit.astype(bf16), jnp.where(earlier, 1.0, 0.0).astype(bf16), preferred_element_type=f32
+    )
+    raised = [jnp.exp(jnp.sum(jnp.where(p, logits, 0.0), axis=0, keepdims=True)) for p in picked]
+    share = 1.0 / sum(raised)
+    line = lax.broadcasted_iota(jnp.int32, (quiet, half), 0)
+    note = jnp.zeros(line.shape, f32)
+    for k in range(top_count):
+        slot = jnp.sum(jnp.where(picked[k], before, 0.0), axis=0, keepdims=True)
+        note = jnp.where(line == k, raised[k] * share, note)
+        note = jnp.where(line == top_count + k, ids[k : k + 1, :].astype(f32), note)
+        note = jnp.where(line == 2 * top_count + k, slot, note)
+    rest = jnp.transpose(jnp.broadcast_to(scale, (half, 128)))[:1, :]
+    for k in range(3):
+        term = rest.astype(bf16).astype(f32)
+        note = jnp.where(line == 3 * top_count + k, term, note)
+        rest = rest - term
+    r.notes[me, :quiet] = note.astype(bf16)
+
+    def take(slot):
+        own_expert = me.astype(f32)
+        note = r.notes[slot, :quiet].astype(f32)
+        r.rows_b[slot, : half // 2, edge:] = r.notes[slot, quiet:, :64]
+        r.rows_b[slot, half // 2 :, edge:] = r.notes[slot, quiet:, 64:]
+        gate = jnp.zeros((1, half), f32)
+        where_to = jnp.full((1, half), -1.0, f32)
+        for k in range(top_count):
+            chosen = note[top_count + k : top_count + k + 1, :] == own_expert
+            gate = jnp.where(chosen, note[k : k + 1, :], gate)
+            where_to = jnp.where(chosen, note[2 * top_count + k : 2 * top_count + k + 1, :], where_to)
+        at = 3 * top_count
+        scales = note[at : at + 1, :] + note[at + 1 : at + 2, :] + note[at + 2 : at + 3, :]
+        match = lax.broadcasted_iota(jnp.int32, (capacity, half), 0).astype(f32) == where_to
+        select = jnp.where(match, 1.0, 0.0).astype(bf16)
+        gates = lax.dot_general(
+            jnp.broadcast_to(gate, (8, half)).astype(bf16), select, across_lanes,
+            preferred_element_type=f32,
+        )
+        r.gate_rows[slot] = gates[:1, :]
+        scales = jnp.sum(jnp.where(match, scales, 0.0), axis=1, keepdims=True)
+        r.out[slot, :, cut:] = jnp.dot(
+            select, r.rows_b[slot], preferred_element_type=f32
+        ).astype(bf16)
+        r.out[slot, :, :cut] = (
+            jnp.dot(select, r.rows_a[slot], preferred_element_type=f32)
+            * scales * mlp[:cut][None, :]
+        ).astype(bf16)
+
+    own_sends(marks)
+    own_sends(slow)
+    advance(fast, 3)
+    take(me)
+
+    def ring_task(way, step):
+        return lambda: take(origin(way, step))
+
+    def pair_task(ways, step):
+        def run():
+            for group in (fast, slow, marks):
+                pair_wait(group, ways[0], step)
+            take(origin(ways[0], step) + flip)
+        return run
+
+    def partner_task():
+        for group in (fast, slow, marks):
+            pair_wait(group, 1, 0)
+        take(partner)
+
+    tasks.append(partner_task)
+    for step in range(1, hops + 1):
+        advance(marks, step)
+        advance(slow, step)
+        if step == 1:
+            advance(fast, 4)
+        for ways in ((1,), (-1,)) if step < hops else ((1, -1),):
+            tasks.append(ring_task(ways[0], step))
+            tasks.append(pair_task(ways, step))
+    while tasks:
+        tasks.pop(0)()
+    r.gates[...] = r.gate_rows[:, 0, :].astype(bf16)
+
+    for group in range(marks + 1):
+        landed(blocks(group, chips - 1), r.ring_send.at[group])
+        landed(blocks(group, chips), r.pair_send.at[group])
+    for index in range(swaps):
+        swap_copy(index).wait_send()
+
+
+def layer_call(
+    tokens, segments, expert_ids, gain, sinks, adam, router_weight, router_bias, mlp_gain,
+    heads, kv_heads, sources, experts, capacity,
+):
+    rows, width = tokens.shape
+    half = rows // 2
+    chips = sources // 2
+    hops = chips // 2
+    q_block, o_block = adam[0].shape[0], adam[4].shape[0]
+    top_count = expert_ids.shape[1]
+    cut = width * 3 // 8 // 128 * 128
+    segments_o = ((0, cut), (cut, cut), (2 * cut, width - 2 * cut))
+    tiles = q_block // 16
+    q_spans = [(16 * t, 16, 1 if t < (tiles + 1) // 2 else -1) for t in range(tiles)]
+    o_spans = [(0, o_block // 2, 1), (o_block // 2, o_block // 2, -1)]
+    last_spans = [(0, 16, 1), (16, o_block - 16, -1)]
+    quarter = half // 4
+    r_spans = [(quarter * t, quarter, 1 if t < 2 else -1) for t in range(4)]
+    tops = (q_block + 31) // 32 * 16, o_block // 2
+    tail_rows, note_rows = sum(tops), 16 + half // 2
+
+    def two_spans(count):
+        first = (count + 31) // 32 * 16
+        return [(0, first, 1), (first, count - first, -1)]
+
+    spans = (
+        q_spans, two_spans(tail_rows), o_spans, o_spans, last_spans, r_spans, r_spans,
+        two_spans(note_rows),
+    )
+    plan, total = piece_plan(spans, hops)
+    cosine, sine = split_tables(rows)
+    bf16, f32 = jnp.bfloat16, jnp.float32
+    hbm = dict(
+        tok=tokens.T, adam=adam,
+        small=[
+            gain, mlp_gain, segments[None, :], jnp.asarray(cosine), jnp.asarray(sine),
+            router_weight.T, router_bias[None, :], expert_ids.T, sinks,
+        ],
+    )
+    small = [pltpu.VMEM(v.shape, v.dtype) for v in hbm["small"][:-1]]
+    dma = pltpu.SemaphoreType.DMA
+    groups, swaps = len(spans), len(segments_o)
+    scratch = dict(
+        tok=pltpu.VMEM(tokens.shape, bf16),
+        tok_t=pltpu.VMEM((width, rows), bf16),
+        small=small + [pltpu.SMEM(sinks.shape, sinks.dtype)],
+        mask=pltpu.VMEM((rows, rows), f32),
+        q_in=pltpu.VMEM((4, q_block, width), f32),
+        o_in=pltpu.VMEM((4, o_block, width), f32),
+        normed=pltpu.VMEM((rows, width), bf16),
+        w_q=pltpu.VMEM((sources * q_block, width), bf16),
+        tails=pltpu.VMEM((sources, tail_rows, 128), bf16),
+        o_part=[pltpu.VMEM((sources * o_block, size), bf16) for _, size in segments_o],
+        proj=pltpu.VMEM((rows, sources * q_block), f32),
+        att=pltpu.VMEM((rows, heads * HEAD_DIM), bf16),
+        res=pltpu.VMEM((half, width), f32),
+        swap_out=[pltpu.VMEM((half, size), bf16) for _, size in segments_o],
+        swap_in=[pltpu.VMEM((half, size), bf16) for _, size in segments_o],
+        rows_a=pltpu.VMEM((sources, half, cut), bf16),
+        rows_b=pltpu.VMEM((sources, half, width - cut), bf16),
+        notes=pltpu.VMEM((sources, note_rows, half), bf16),
+        gate_rows=pltpu.VMEM((sources, 1, capacity), f32),
+        load_sem=dma((tiles + 11,)),
+        ring_send=dma((groups,)),
+        ring_recv=dma((total,)),
+        pair_send=dma((groups,)),
+        pair_recv=dma((groups - 3 + 3 * chips,)),
+        swap_send=dma((swaps,)),
+        swap_recv=dma((swaps,)),
+    )
+    results = dict(
+        out=pltpu.VMEM((sources, capacity, width), bf16),
+        gates=pltpu.VMEM((sources, capacity), bf16),
+    )
+    operands, hbm_tree = jax.tree.flatten(hbm)
+    outputs, result_tree = jax.tree.flatten(results)
+    buffers, scratch_tree = jax.tree.flatten(scratch)
+    own = (q_block, tail_rows, *[o_block] * swaps, half, half, note_rows)
+    cfg = types.SimpleNamespace(
+        plan=plan, own=own, chips=chips, heads=heads, kv_heads=kv_heads, segments=segments_o,
+        top_count=top_count, tops=tops,
+    )
+
+    def body(*refs):
+        taken = list(refs)
+        spaces = []
+        for tree in (hbm_tree, result_tree, scratch_tree):
+            count = tree.num_leaves
+            spaces.append(jax.tree.unflatten(tree, taken[:count]))
+            taken = taken[count:]
+        layer_kernel(
+            cfg, types.SimpleNamespace(**spaces[0]),
+            types.SimpleNamespace(**spaces[1], **spaces[2]),
+        )
+
+    gates, out = pl.pallas_call(
+        body,
+        out_shape=outputs,
+        in_specs=[pl.BlockSpec(memory_space=pltpu.HBM)] * len(operands),
+        out_specs=[pl.BlockSpec(memory_space=pltpu.VMEM)] * 2,
+        scratch_shapes=buffers,
+        compiler_params=pltpu.CompilerParams(
+            collective_id=4, has_side_effects=True, vmem_limit_bytes=48 * 1024 * 1024
+        ),
+        name="layer",
+    )(*(pltpu.with_memory_space_constraint(v, pltpu.HBM) for v in operands))
+    return out, gates
+
+
+def layer_fits(tokens, adam, sources, experts, capacity, groups):
+    rows, width = tokens.shape
+    return (
+        groups == 2 and experts == sources and sources == 16 and rows == 256
+        and adam[0].shape[0] % 16 == 0 and adam[4].shape[0] % 32 == 0
+        and width % 128 == 64 and width >= 1024 and capacity <= 128
+    )
+
+
 def on_device(
     tokens,
     segment_ids,
@@ -476,6 +1066,13 @@
     experts = router_weight.shape[1]
     top_count = expert_ids.shape[1]
     capacity = 2 * half * top_count // experts
+    adam = [qkv_master, qkv_mom, qkv_var, qkv_grad, o_master, o_mom, o_var, o_grad]
+    if layer_fits(tokens, adam, sources, experts, capacity, lax.axis_size("dp")):
+        dispatched, gate_slots = layer_call(
+            tokens, segment_ids, expert_ids, attn_gain, sinks, adam, router_weight, router_bias,
+            mlp_gain, heads_here, kv_here, sources, experts, capacity,
+        )
+        return (dispatched[None, :, None], gate_slots[None, :, None])
     qkv_local = adam_weights(qkv_master, qkv_mom, qkv_var, qkv_grad)
     o_local = adam_weights(o_master, o_mom, o_var, o_grad)
     qkv_full, o_full = gather_rows([qkv_local, o_local], sources, 1)

time: 191 us -> 134 us (0.70)
  Pallas kernels: 166 us -> 129 us
  local copies, waits for them, and re-layouts: 18.1 us -> 3.21 us
  other arithmetic: 5.87 us -> 0 us
    pallas_call x5 -> x1, Pallas kernels: 166 us -> 129 us  [layer_call(): pl.pallas_call(body, out_shape=outputs, in_specs=[pl.BlockSpec(memory_spa...]
    unnamed x32 -> x2, local copies, waits for them, and re-layouts: 18 us -> 3.21 us
    convert_element_type x3 -> x0, other arithmetic: 5.05 us -> none  [the longest x2 5.05 us: adam_weights(): return (master - learn_rate * update).astype(jnp.bfloat16)]
where the time goes in v1:
time: 134 us; the launch traced here: 133 us
  Pallas kernels  129 us (96%)
  local copies, waits for them, and re-layouts  3.21 us (2%)
    pallas_call x1, Pallas kernels, layer_call(): pl.pallas_call(body, out_shape=outputs, in_specs=[pl.BlockSpec(memory_spa...  129 us
    unnamed x2, local copies, waits for them, and re-layouts  3.21 us

profile of v1, /device:TPU:1, one launch (start us, length us, event | category | flops | bytes accessed | tf_op | source)
XLA Modules:
  0.0 132.9 jit_solution(718762966132973400)
XLA Ops:
  0.6 129.1 %layer.1 = (bf16[16,64]{1,0:T(8,128)(2,1)S(1)}, bf16[16,64,2880]{2,1,0:T(8,128)(2,1)S(1)}) custom-call(f32[80,2880]{1,0:T(8,128)} %refs_0_.1, f32[80,2880]{1,0:T(8,128)} %refs_1_.1, f32[80,2880]{1,0:T(8,128)} %refs_2_.1, f32[80,2880]{1,0:T(8,128)} %refs_3_.1, f32[64,2880]{1,0:T(8,128)} %refs_4_.1, f32[64,2880]{1,0:T(8,128)} %refs_5_.1, f32[64,2880]{1,0:T(8,128)} %refs_6_.1, ...), custom_call_target="tpu_custom_call" | custom-call | tf_op jit(solution)/shard_map/layer/pallas_call | solution.py:1020
  129.7 2.6 %copy.23 = bf16[1,16,1,64,2880]{4,3,2,1,0:T(8,128)(2,1)} copy(bf16[1,16,1,64,2880]{4,3,2,1,0:T(8,128)(2,1)S(1)} %bitcast.9) | data formatting | bytes 11796480
  132.3 0.6 copy.24

commit v2 on v1

--- a/solution.py
+++ b/solution.py
@@ -523,7 +523,6 @@
     for other in (left, right, partner):
         pl.semaphore_signal(barrier, inc=1, device_id={"expert": other}, device_id_type=MESH)
     pl.semaphore_signal(barrier, inc=1, device_id={"dp": across}, device_id_type=MESH)
-    pl.semaphore_wait(barrier, 4)
 
     swaps = len(cfg.segments)
     fast, slow, marks = swaps + 2, swaps + 3, swaps + 4
@@ -627,11 +626,12 @@
         at, lanes = (start, 0) if start < upper else (start - upper, 64)
         r.tails[me, at : at + 16, lanes : lanes + 64] = fresh[:, full:]
 
-    starts = list(range(0, q_block, 16))
-    for index, start in enumerate(starts):
+    starts_done = {start + size: (start,) for group, start, size, *_ in plan if group == 0}
+    for start in range(0, q_block, 16):
         adam_qkv(start)
-        if index:
-            own_sends(0, starts[index - 1 : index], False)
+        if start == 16:
+            pl.semaphore_wait(barrier, 4)
+        own_sends(0, starts_done.get(start, ()), False)
     ready("o", r.o_in)
     first = pl.multiple_of(me * o_block, 16)
     for part, (start, size) in zip(r.o_part, cfg.segments):
@@ -640,7 +640,7 @@
     lower = o_block // 2
     r.tails[me, upper:, :64] = fresh[:lower, size - 64 :]
     r.tails[me, upper:, 64:] = fresh[lower:, size - 64 :]
-    own_sends(0, starts[-1:])
+    own_sends(0, starts_done[q_block])
     own_sends(1)
     ready("tok", r.tok_t)
     for start in range(0, width, 128):
@@ -785,9 +785,9 @@
     for slab in range(heads_slabs // 2, heads_slabs):
         attend(slab)
     advance(2, hops)
+    advance(4, 1)
     all_here(2)
     swap(0)
-    advance(4, 1)
     advance(3, 2)
     advance(4, 2)
     advance(3, 3)
@@ -922,6 +922,31 @@
         swap_copy(index).wait_send()
 
 
+def write_kernel(pieces, out_ref, gate_ref, out_hbm, gate_hbm, sems):
+    share = out_ref.shape[0] // pieces
+    copies = [pltpu.make_async_copy(gate_ref, gate_hbm, sems.at[pieces])]
+    for piece in range(pieces):
+        part = pl.ds(piece * share, share)
+        copies.append(pltpu.make_async_copy(out_ref.at[part], out_hbm.at[part], sems.at[piece]))
+    for copy in copies:
+        copy.start()
+    for copy in copies:
+        copy.wait()
+
+
+def write_call(out, gates, pieces):
+    vmem, hbm = (pl.BlockSpec(memory_space=kind) for kind in (pltpu.VMEM, pltpu.HBM))
+    return pl.pallas_call(
+        functools.partial(write_kernel, pieces),
+        out_shape=[pltpu.HBM(v.shape, v.dtype) for v in (out, gates)],
+        in_specs=[vmem] * 2,
+        out_specs=[hbm] * 2,
+        scratch_shapes=[pltpu.SemaphoreType.DMA((pieces + 1,))],
+        compiler_params=pltpu.CompilerParams(vmem_limit_bytes=2 * 1024 * 1024),
+        name="write_out",
+    )(out, gates)
+
+
 def layer_call(
     tokens, segments, expert_ids, gain, sinks, adam, router_weight, router_bias, mlp_gain,
     heads, kv_heads, sources, experts, capacity,
@@ -935,7 +960,8 @@
     cut = width * 3 // 8 // 128 * 128
     segments_o = ((0, cut), (cut, cut), (2 * cut, width - 2 * cut))
     tiles = q_block // 16
-    q_spans = [(16 * t, 16, 1 if t < (tiles + 1) // 2 else -1) for t in range(tiles)]
+    top = (tiles + 1) // 2 * 16
+    q_spans = [(0, 32, 1), (32, top - 32, 1), (top, q_block - top, -1)]
     o_spans = [(0, o_block // 2, 1), (o_block // 2, o_block // 2, -1)]
     last_spans = [(0, 16, 1), (16, o_block - 16, -1)]
     quarter = half // 4
@@ -943,13 +969,9 @@
     tops = (q_block + 31) // 32 * 16, o_block // 2
     tail_rows, note_rows = sum(tops), 16 + half // 2
 
-    def two_spans(count):
-        first = (count + 31) // 32 * 16
-        return [(0, first, 1), (first, count - first, -1)]
-
     spans = (
-        q_spans, two_spans(tail_rows), o_spans, o_spans, last_spans, r_spans, r_spans,
-        two_spans(note_rows),
+        q_spans, [(0, tail_rows, -1)], o_spans, o_spans, last_spans, r_spans, r_spans,
+        [(0, note_rows, 1)],
     )
     plan, total = piece_plan(spans, hops)
     cosine, sine = split_tables(rows)
@@ -1028,14 +1050,14 @@
         ),
         name="layer",
     )(*(pltpu.with_memory_space_constraint(v, pltpu.HBM) for v in operands))
-    return out, gates
+    return write_call(out, gates, 8)
 
 
 def layer_fits(tokens, adam, sources, experts, capacity, groups):
     rows, width = tokens.shape
     return (
         groups == 2 and experts == sources and sources == 16 and rows == 256
-        and adam[0].shape[0] % 16 == 0 and adam[4].shape[0] % 32 == 0
+        and adam[0].shape[0] % 16 == 0 and adam[0].shape[0] >= 80 and adam[4].shape[0] % 32 == 0
         and width % 128 == 64 and width >= 1024 and capacity <= 128
     )
 

time: 134 us -> 132 us (0.985)
  local copies, waits for them, and re-layouts: 3.21 us -> 0 us
  Pallas kernels: 129 us -> 131 us
    unnamed x2 -> x0, local copies, waits for them, and re-layouts: 3.21 us -> none
    pallas_call x0 -> x1, Pallas kernels: none -> 2.67 us  [write_call(): pl.pallas_call(functools.partial(write_kernel, pieces), out_shape=[pltpu....]
where the time goes in v2:
time: 132 us
  Pallas kernels  131 us (99%)
    pallas_call x1, Pallas kernels, layer_call(): pl.pallas_call(body, out_shape=outputs, in_specs=[pl.BlockSpec(memory_spa...  128 us
    pallas_call x1, Pallas kernels, write_call(): pl.pallas_call(functools.partial(write_kernel, pieces), out_shape=[pltpu....  2.67 us

profile of v2, /device:TPU:1, one launch (start us, length us, event | category | flops | bytes accessed | tf_op | source)
XLA Modules:
  0.0 131.6 jit_solution(15796066970775196810)
XLA Ops:
  0.6 128.1 %layer.1 = (bf16[16,64]{1,0:T(8,128)(2,1)S(1)}, bf16[16,64,2880]{2,1,0:T(8,128)(2,1)S(1)}) custom-call(f32[80,2880]{1,0:T(8,128)} %refs_0_.1, f32[80,2880]{1,0:T(8,128)} %refs_1_.1, f32[80,2880]{1,0:T(8,128)} %refs_2_.1, f32[80,2880]{1,0:T(8,128)} %refs_3_.1, f32[64,2880]{1,0:T(8,128)} %refs_4_.1, f32[64,2880]{1,0:T(8,128)} %refs_5_.1, f32[64,2880]{1,0:T(8,128)} %refs_6_.1, ...), custom_call_target="tpu_custom_call" | custom-call | tf_op jit(solution)/shard_map/layer/pallas_call | solution.py:1042
  128.8 2.7 %write_out.1 = (bf16[16,64,2880]{2,1,0:T(8,128)(2,1)}, bf16[16,64]{1,0:T(8,128)(2,1)}) custom-call(bf16[16,64,2880]{2,1,0:T(8,128)(2,1)S(1)} %get-tuple-element.6.out_ref, bf16[16,64]{1,0:T(8,128)(2,1)S(1)} %get-tuple-element.7.gate_ref), custom_call_target="tpu_custom_call" | custom-call | tf_op jit(solution)/shard_map/write_out/pallas_call | solution.py:939

commit v3 on v2

--- a/solution.py
+++ b/solution.py
@@ -961,7 +961,7 @@
     segments_o = ((0, cut), (cut, cut), (2 * cut, width - 2 * cut))
     tiles = q_block // 16
     top = (tiles + 1) // 2 * 16
-    q_spans = [(0, 32, 1), (32, top - 32, 1), (top, q_block - top, -1)]
+    q_spans = [(0, 16, 1), (16, top - 16, 1), (top, q_block - top, -1)]
     o_spans = [(0, o_block // 2, 1), (o_block // 2, o_block // 2, -1)]
     last_spans = [(0, 16, 1), (16, o_block - 16, -1)]
     quarter = half // 4

time: 132 us -> 132 us (level)
  no operation moved by 1% of the time
where the time goes in v3:
time: 132 us; the launch traced here: 131 us
  Pallas kernels  131 us (99%)
    pallas_call x1, Pallas kernels, layer_call(): pl.pallas_call(body, out_shape=outputs, in_specs=[pl.BlockSpec(memory_spa...  128 us
    pallas_call x1, Pallas kernels, write_call(): pl.pallas_call(functools.partial(write_kernel, pieces), out_shape=[pltpu....  2.67 us

profile of v3, /device:TPU:1, one launch (start us, length us, event | category | flops | bytes accessed | tf_op | source)
XLA Modules:
  0.0 131.4 jit_solution(12693757229390206080)
XLA Ops:
  0.6 127.9 %layer.1 = (bf16[16,64]{1,0:T(8,128)(2,1)S(1)}, bf16[16,64,2880]{2,1,0:T(8,128)(2,1)S(1)}) custom-call(f32[80,2880]{1,0:T(8,128)} %refs_0_.1, f32[80,2880]{1,0:T(8,128)} %refs_1_.1, f32[80,2880]{1,0:T(8,128)} %refs_2_.1, f32[80,2880]{1,0:T(8,128)} %refs_3_.1, f32[64,2880]{1,0:T(8,128)} %refs_4_.1, f32[64,2880]{1,0:T(8,128)} %refs_5_.1, f32[64,2880]{1,0:T(8,128)} %refs_6_.1, ...), custom_call_target="tpu_custom_call" | custom-call | tf_op jit(solution)/shard_map/layer/pallas_call | solution.py:1042
  128.6 2.7 %write_out.1 = (bf16[16,64,2880]{2,1,0:T(8,128)(2,1)}, bf16[16,64]{1,0:T(8,128)(2,1)}) custom-call(bf16[16,64,2880]{2,1,0:T(8,128)(2,1)S(1)} %get-tuple-element.6.out_ref, bf16[16,64]{1,0:T(8,128)(2,1)S(1)} %get-tuple-element.7.gate_ref), custom_call_target="tpu_custom_call" | custom-call | tf_op jit(solution)/shard_map/write_out/pallas_call | solution.py:939
